TPU v7x, 32 devices: a whole 2x2x4 slice. The times are simulated.
32 devices in a mesh: outer: 4 (over y, x), inner: 8 (over z, core).
Axes of the slice: x: 2, y: 2, z: 4, core: 2. Of those that a mesh axis runs over, the one named last changes fastest.
Arguments:
- tokens: bfloat16 [4096, 4096], P('inner', 'outer'), may hold values from -6 to 6
- cotangent: bfloat16 [4096, 4096], P('inner', 'outer'), may hold values from -0.09375 to 0.09375
- weight_cache: bfloat16 [4096, 4096], P(None, 'outer'), may hold values from -0.09375 to 0.09375
- weight_delta: bfloat16 [4096, 4096], P('inner', 'outer'), may hold values from -0.078125 to 0.078125
- sign_bits: int32 [4096], P('outer'), may hold values from 0 to 1
- master: float32 [4096, 4096], P('inner', 'outer'), may hold values from -1.5 to 1.5
- moment: float32 [4096, 4096], P('inner', 'outer'), may hold values from -6 to 6
- variance: float32 [4096, 4096], P('inner', 'outer'), may hold values from 0.25 to 4
Outputs:
- activation: float32 [4096, 4096], P('inner', 'outer')
- new_master: float32 [4096, 4096], P('inner', 'outer')
- new_moment: float32 [4096, 4096], P('inner', 'outer')
- new_variance: float32 [4096, 4096], P('inner', 'outer')
- block_scales: float32 [4096, 32], P('inner', 'outer')
All inputs are finite; a program needn't handle non-finite values.
Results may differ from a plain program's by a relative error of at most 0.003.
Values may be sent and summed in bfloat16 or wider, within the bound.
No kernel may reach another device: no remote copies, remote signals or barrier semaphores. Data moves between devices by JAX's collectives and lax.ppermute only.
A program may use at most 128 MiB of HBM per device.

v0:
```python
import jax
import jax.numpy as jnp
from jax import lax
from jax.sharding import PartitionSpec as P

BLOCK = 128


def hadamard_table(length):
    first = jnp.arange(length, dtype=jnp.int32)[:, None]
    second = jnp.arange(length, dtype=jnp.int32)[None, :]
    common = jnp.bitwise_and(first, second)
    parity = jnp.zeros((length, length), jnp.int32)
    for place in range(length.bit_length() - 1):
        parity = parity + jnp.bitwise_and(jnp.right_shift(common, place), 1)
    return (1 - 2 * (parity % 2)).astype(jnp.float32) / jnp.sqrt(jnp.float32(length))


def smooth(values, signs, table):
    height = values.shape[0]
    blocks = values.reshape(height, -1, table.shape[0]) * signs.reshape(-1, table.shape[0])
    mixed = jnp.einsum("rbk,kj->rbj", blocks, table, precision=lax.Precision.HIGHEST)
    return mixed.reshape(height, -1)


def unsmooth(values, signs, table):
    height = values.shape[0]
    blocks = values.reshape(height, -1, table.shape[0])
    mixed = jnp.einsum("rbj,jk->rbk", blocks, table, precision=lax.Precision.HIGHEST)
    return (mixed * signs.reshape(-1, table.shape[0])).reshape(height, -1)


def outer_product(left, right):
    return lax.dot_general(
        left, right, (((0,), (0,)), ((), ())), preferred_element_type=jnp.float32
    )


def body(tokens, cotangent, weight_cache, weight_delta, sign_bits, master, moment, variance):
    table = hadamard_table(BLOCK)
    signs = (1 - 2 * sign_bits).astype(jnp.float32)
    shard_rows = master.shape[0]
    gathered = lax.all_gather(tokens, "outer", axis=1, tiled=True)
    merged = (
        weight_cache.astype(jnp.float32)
        + lax.all_gather(weight_delta, "inner", axis=0, tiled=True).astype(jnp.float32)
    ).astype(jnp.bfloat16)
    columns = gathered
    output = jnp.dot(columns, merged, preferred_element_type=jnp.float32)
    columns = gathered
    partial_value = outer_product(columns, cotangent)
    summed = lax.psum_scatter(
        smooth(partial_value, signs, table), "inner", scatter_dimension=0, tiled=True
    )
    block_scales = jnp.max(jnp.abs(summed.reshape(shard_rows, -1, BLOCK)), axis=2)
    restored = unsmooth(summed, signs, table)
    new_moment = 0.9 * moment + 0.1 * restored
    new_variance = 0.95 * variance + 0.05 * restored * restored
    corrected = new_moment / (1.0 - 0.9**10)
    spread = jnp.sqrt(new_variance / (1.0 - 0.95**10)) + 1e-08
    new_master = master - 0.01 * (corrected / spread + 0.1 * master)
    return (output, new_master, new_moment, new_variance, block_scales)


def solution(mesh):
    placed = (
        P("inner", "outer"),
        P("inner", "outer"),
        P(None, "outer"),
        P("inner", "outer"),
        P("outer"),
        P("inner", "outer"),
        P("inner", "outer"),
        P("inner", "outer"),
    )
    return jax.shard_map(
        body,
        mesh=mesh,
        in_specs=placed,
        out_specs=(
            P("inner", "outer"),
            P("inner", "outer"),
            P("inner", "outer"),
            P("inner", "outer"),
            P("inner", "outer"),
        ),
        check_vma=False,
    )
```

profile of v0, /device:TPU:0, one launch (start us, length us, event | category | flops | bytes accessed | tf_op | source)
XLA Modules:
  0.0 339.3 jit_solution(2101183331217404971)
XLA Ops:
  7.2 0.0 copy-start
  7.2 0.0 copy-start.3
  7.2 0.0 all-gather.5.cloned.1.call-start
  7.2 0.7 all-gather.5.cloned.1.call-update
  7.9 0.0 all-gather.3.cloned.1.call-start
  8.0 0.7 all-gather.3.cloned.1.call-update
  8.7 0.0 reduce-scatter.2.cloned.1.call-start
  8.7 0.0 copy-done.3
  8.7 56.4 %all-gather.5.cloned.1.call-done = bf16[512,4096]{1,0:T(8,128)(2,1)} async-done(((bf16[512,1024]{1,0:T(8,128)(2,1)}), bf16[512,4096]{1,0:T(8,128)(2,1)}) %all-gather.5.cloned.1.call-update) | async-done | bytes 4194320 | tf_op jit(solution)/shard_map/all_gather | solution.py:43
  65.2 0.0 copy-done
  65.2 11.0 %fusion.47 = f32[4096,1024]{0,1:T(8,128)} fusion(bf16[512,4096]{1,0:T(8,128)(2,1)} %all-gather.5.cloned.1.call-done, bf16[512,1024]{1,0:T(8,128)(2,1)S(1)} %copy-done), kind=kOutput, calls=%fused_computation.54 | convolution fusion | flops 4294967296 | bytes 22020096 | tf_op jit(solution)/shard_map/dot_general | solution.py:34
  76.2 17.8 %copy.18 = f32[4096,8,128]{2,0,1:T(8,128)} copy(f32[4096,8,128]{0,2,1:T(8,128)} %bitcast.18) | data formatting | bytes 33554432 | tf_op jit(solution)/shard_map/reshape | solution.py:21
  93.9 22.9 %fusion = f32[4096,8,128]{0,2,1:T(8,128)} fusion(f32[4096,8,128]{2,0,1:T(8,128)} %copy.18, f32[8,128]{1,0:T(8,128)S(1)} %convert_bitcast_fusion), kind=kOutput, calls=%fused_computation | convolution fusion | flops 6447235072 | bytes 33558528 | tf_op jit(solution)/shard_map/rbk,kj->rbj/dot_general | solution.py:22
  116.9 0.0 reduce-scatter.2.cloned.1.call-update
  116.9 31.9 %all-gather.3.cloned.1.call-done = bf16[4096,1024]{1,0:T(8,128)(2,1)} async-done(((bf16[512,1024]{1,0:T(8,128)(2,1)}), bf16[4096,1024]{1,0:T(8,128)(2,1)}) %all-gather.3.cloned.1.call-update) | async-done | bytes 8388624 | tf_op jit(solution)/shard_map/all_gather | solution.py:46
  148.8 9.6 %fusion.5 = f32[512,1024]{0,1:T(8,128)S(1)} fusion(bf16[512,4096]{1,0:T(8,128)(2,1)} %all-gather.5.cloned.1.call-done, bf16[4096,1024]{1,0:T(8,128)(2,1)} %all-gather.3.cloned.1.call-done, bf16[4096,1024]{1,0:T(8,128)(2,1)} %param.10), kind=kOutput, calls=%fused_computation.10 | convolution fusion | flops 4311744512 | bytes 23068672 | tf_op jit(solution)/shard_map/dot_general | solution.py:49
  158.5 1.8 copy.23
  160.3 157.6 %reduce-scatter.2.cloned.1.call-done = f32[512,1024]{0,1:T(8,128)} async-done(((f32[4096,1024]{0,1:T(8,128)}), f32[512,1024]{0,1:T(8,128)}) %reduce-scatter.2.cloned.1.call-update) | async-done | bytes 2097168 | tf_op jit(solution)/shard_map/reduce_scatter | solution.py:52
  317.9 5.2 %convolution_multiply_fusion = f32[512,8,128]{0,2,1:T(8,128)} fusion(f32[512,8,128]{0,2,1:T(8,128)} %bitcast.19, f32[8,128]{1,0:T(8,128)S(1)} %convert_bitcast_fusion), kind=kOutput, calls=%fused_computation.11 | convolution fusion | flops 806420480 | bytes 4198400 | tf_op jit(solution)/shard_map/rbj,jk->rbk/dot_general | solution.py:29
  323.1 1.9 copy.20
  325.0 0.0 copy-start.2
  325.0 0.0 copy-start.1
  325.0 6.9 %multiply_subtract_fusion = (f32[512,1024]{1,0:T(8,128)}, f32[512,1024]{1,0:T(8,128)}, f32[512,1024]{1,0:T(8,128)}) fusion(f32[512,1024]{1,0:T(8,128)} %param.13, f32[512,1024]{1,0:T(8,128)S(1)} %copy.20, f32[512,1024]{1,0:T(8,128)} %param.14, f32[512,1024]{1,0:T(8,128)} %param.15), kind=kLoop, calls=%fused_computation.8 | loop fusion | flops 7864320 | bytes 14680064 | tf_op jit(solution)/shard_map/sub | solution.py:61
  331.9 0.0 copy-done.2
  331.9 0.9 abs_reduce_fusion
  332.8 0.0 copy-done.1
  (1 shorter events, 0.0 us)
Async XLA Ops:
  7.2 58.0 %copy-start = (bf16[512,1024]{1,0:T(8,128)(2,1)S(1)}, bf16[512,1024]{1,0:T(8,128)(2,1)}, u32[]{:S(2)}) copy-start(bf16[512,1024]{1,0:T(8,128)(2,1)} %param.9) | copy-start | bytes 3145732
  7.2 1.5 copy-start.3
  7.2 58.0 %all-gather.5.cloned.1.call-start = ((), (), s32[]{:S(2)}) async-start(), calls=%async_computation.2 | async-start | bytes 5242880 | tf_op jit(solution)/shard_map/all_gather | solution.py:43
  7.9 140.9 %all-gather.3.cloned.1.call-start = ((), (), s32[]{:S(2)}) async-start(), calls=%async_computation.1 | async-start | bytes 9437184 | tf_op jit(solution)/shard_map/all_gather | solution.py:46
  8.7 309.2 %reduce-scatter.2.cloned.1.call-start = ((), (), s32[]{:S(2)}) async-start(), calls=%async_computation.3 | async-start | bytes 18874368 | tf_op jit(solution)/shard_map/reduce_scatter | solution.py:52
  325.0 6.9 %copy-start.2 = (f32[512,1024]{0,1:T(8,128)S(1)}, f32[512,1024]{0,1:T(8,128)}, u32[]{:S(2)}) copy-start(f32[512,1024]{0,1:T(8,128)} %reduce-scatter.2.cloned.1.call-done) | copy-start | bytes 6291460
  325.0 7.8 %copy-start.1 = (bf16[512,1024]{1,0:T(8,128)(2,1)S(1)}, bf16[512,1024]{1,0:T(8,128)(2,1)}, u32[]{:S(2)}) copy-start(bf16[512,1024]{1,0:T(8,128)(2,1)} %param.9) | copy-start | bytes 3145732
Sparse Core Ops, SparseCore 0:
  9.8 55.2 all-gather.4
  66.8 82.0 all-gather.2
  151.2 166.6 reduce-scatter.1
where the time goes:
time: 340 us; the launch traced here: 339 us
  waiting for transfers between devices  247 us (73%)
  matrix products  48.7 us (14%)
  local copies, waits for them, and re-layouts  21.5 us (6%)
  between operations  13.8 us (4%)
  other arithmetic  7.74 us (2%)
    reduce_scatter x1, waiting for transfers between devices, body(): lax.psum_scatter(smooth(partial_value, signs, table), 'inner', scatter_di...  158 us
    all_gather x1, waiting for transfers between devices, body(): gathered = lax.all_gather(tokens, 'outer', axis=1, tiled=True)  56.4 us
    all_gather x1, waiting for transfers between devices, body(): lax.all_gather(weight_delta, 'inner', axis=0, tiled=True)  31.9 us
    dot_general x1, matrix products, smooth(): jnp.einsum('rbk,kj->rbj', blocks, table, precision=lax.Precision.HIGHEST)  22.9 us
    reshape x1, local copies, waits for them, and re-layouts, smooth(): values.reshape(height, -1, table.shape[0])  17.8 us
    dot_general x1, matrix products, outer_product(): lax.dot_general(left, right, (((0,), (0,)), ((), ())), preferred_element_...  11 us
    dot_general x1, matrix products, body(): output = jnp.dot(columns, merged, preferred_element_type=jnp.float32)  9.64 us
    sub x1, other arithmetic, body(): new_master = master - 0.01 * (corrected / spread + 0.1 * master)  6.87 us
  transfers between devices with their start and end apart: 3, of which 3 were waited for; matrix products, arithmetic and copies ran while one was open for 19% of the time, Pallas kernels for 0%

commit v1 on v0

--- a/solution.py
+++ b/solution.py
@@ -4,6 +4,18 @@
 from jax.sharding import PartitionSpec as P
 
 BLOCK = 128
+
+
+def collect(x, axis, dim):
+    ways, here, step = (lax.axis_size(axis), lax.axis_index(axis), x.shape[dim])
+    line, have = (x, 1)
+    while have < ways:
+        line = jnp.concatenate(
+            [line, lax.ppermute(line, axis, [(d, (d - have) % ways) for d in range(ways)])],
+            axis=dim,
+        )
+        have = 2 * have
+    return jnp.roll(line, here * step, axis=dim)
 
 
 def hadamard_table(length):
@@ -40,7 +52,7 @@
     table = hadamard_table(BLOCK)
     signs = (1 - 2 * sign_bits).astype(jnp.float32)
     shard_rows = master.shape[0]
-    gathered = lax.all_gather(tokens, "outer", axis=1, tiled=True)
+    gathered = collect(tokens, "outer", 1)
     merged = (
         weight_cache.astype(jnp.float32)
         + lax.all_gather(weight_delta, "inner", axis=0, tiled=True).astype(jnp.float32)

time: 340 us -> 329 us (0.968)
  waiting for transfers between devices: 247 us -> 226 us
  starting transfers between devices: 0.11 us -> 5.5 us
    ppermute x0 -> x2, waiting for transfers between devices: none -> 68 us  [collect(): lax.ppermute(line, axis, [(d, (d - have) % ways) for d in range(ways)])]
    all_gather x1 -> x0, waiting for transfers between devices: 56.4 us -> none  [body(): gathered = lax.all_gather(tokens, 'outer', axis=1, tiled=True)]
    all_gather x1, waiting for transfers between devices: 31.9 us -> 0.02 us  [body(): lax.all_gather(weight_delta, 'inner', axis=0, tiled=True)]
    ppermute x0 -> x2, starting transfers between devices: none -> 5.42 us  [collect(): lax.ppermute(line, axis, [(d, (d - have) % ways) for d in range(ways)])]
  transfers between devices with their start and end apart: 3 -> 4, of which waited for: 3 -> 3; matrix products, arithmetic and copies ran while one was open for 19% -> 21% of each run, Pallas kernels for 0% -> 0%
where the time goes in v1:
time: 329 us
  waiting for transfers between devices  226 us (69%)
  matrix products  49.1 us (15%)
  local copies, waits for them, and re-layouts  23.2 us (7%)
  between operations  14.2 us (4%)
  other arithmetic  10.5 us (3%)
  starting transfers between devices  5.5 us (2%)
    reduce_scatter x1, waiting for transfers between devices, body(): lax.psum_scatter(smooth(partial_value, signs, table), 'inner', scatter_di...  158 us
    ppermute x2, waiting for transfers between devices, collect(): lax.ppermute(line, axis, [(d, (d - have) % ways) for d in range(ways)])  68 us
    dot_general x1, matrix products, smooth(): jnp.einsum('rbk,kj->rbj', blocks, table, precision=lax.Precision.HIGHEST)  22.8 us
    reshape x1, local copies, waits for them, and re-layouts, smooth(): values.reshape(height, -1, table.shape[0])  17.4 us
    dot_general x1, matrix products, body(): output = jnp.dot(columns, merged, preferred_element_type=jnp.float32)  12.8 us
    dot_general x1, matrix products, outer_product(): lax.dot_general(left, right, (((0,), (0,)), ((), ())), preferred_element_...  8.29 us
    sub x1, other arithmetic, body(): new_master = master - 0.01 * (corrected / spread + 0.1 * master)  6.87 us
  transfers between devices with their start and end apart: 4, of which 3 were waited for; matrix products, arithmetic and copies ran while one was open for 21% of the time, Pallas kernels for 0%

profile of v1, /device:TPU:0, one launch (start us, length us, event | category | flops | bytes accessed | tf_op | source)
XLA Modules:
  0.0 328.7 jit_solution(13065172695997911572)
XLA Ops:
  7.2 0.0 copy-start
  7.2 0.0 all-gather.2.cloned.1.call-start
  7.2 0.7 all-gather.2.cloned.1.call-update
  7.9 0.0 copy-start.2
  7.9 0.0 reduce-scatter.2.cloned.1.call-start
  8.0 4.0 %collective-permute-start = (bf16[512,1024]{1,0:T(8,128)(2,1)}, bf16[512,1024]{1,0:T(8,128)(2,1)S(1)}, u32[]{:S(2)}, u32[]{:S(2)}) collective-permute-start(bf16[512,1024]{1,0:T(8,128)(2,1)} %param.8), channel_id=1, source_target_pairs={{0,24},{8,0},{16,8},{24,16},{1,25},{9,1},{17,9},{25,17},{2,26},{10... | collective-permute-start | bytes 3145736 | tf_op jit(solution)/shard_map/ppermute | solution.py:14
  11.9 22.7 %collective-permute-done = bf16[512,1024]{1,0:T(8,128)(2,1)S(1)} collective-permute-done((bf16[512,1024]{1,0:T(8,128)(2,1)}, bf16[512,1024]{1,0:T(8,128)(2,1)S(1)}, u32[]{:S(2)}, u32[]{:S(2)}) %collective-permute-start) | collective-permute-done | bytes 1048608 | tf_op jit(solution)/shard_map/ppermute | solution.py:14
  34.7 2.7 pad_maximum_fusion
  37.4 0.0 copy-start.5
  37.4 1.4 collective-permute-start.1
  38.9 0.0 copy-done.2
  38.9 0.1 constant_dynamic-update-slice_fusion.5
  39.0 0.0 copy-done.5
  39.0 0.1 constant_dynamic-update-slice_fusion.4
  39.1 45.2 %collective-permute-done.1 = bf16[512,2048]{1,0:T(8,128)(2,1)} collective-permute-done((bf16[512,2048]{1,0:T(8,128)(2,1)}, bf16[512,2048]{1,0:T(8,128)(2,1)}, u32[]{:S(2)}, u32[]{:S(2)}) %collective-permute-start.1) | collective-permute-done | bytes 2097184 | tf_op jit(solution)/shard_map/ppermute | solution.py:14
  84.3 1.7 constant_dynamic-update-slice_fusion.3
  86.0 0.1 constant_dynamic-update-slice_fusion.2
  86.1 0.1 constant_dynamic-update-slice_fusion.1
  86.2 1.7 constant_dynamic-update-slice_fusion
  88.0 0.0 copy-done
  88.0 0.0 copy-start.4
  88.0 8.3 %fusion.4 = f32[4096,1024]{0,1:T(8,128)} fusion(bf16[512,1024]{1,0:T(8,128)(2,1)S(1)} %copy-done, bf16[512,8192]{1,0:T(8,128)(2,1)S(1)} %constant_dynamic-update-slice_fusion, s32[]{:T(128)S(6)} %select_n.22), kind=kOutput, calls=%fused_computation.5 | convolution fusion | flops 4294967296 | bytes 22020100 | tf_op jit(solution)/shard_map/dot_general | solution.py:46
  96.3 0.0 copy-done.4
  96.3 17.4 %copy.17 = f32[4096,8,128]{2,0,1:T(8,128)} copy(f32[4096,8,128]{0,2,1:T(8,128)} %bitcast.14) | data formatting | bytes 33554432 | tf_op jit(solution)/shard_map/reshape | solution.py:33
  113.7 22.8 %fusion = f32[4096,8,128]{0,2,1:T(8,128)} fusion(f32[4096,8,128]{2,0,1:T(8,128)} %copy.17, f32[8,128]{1,0:T(8,128)S(1)} %convert_bitcast_fusion), kind=kOutput, calls=%fused_computation | convolution fusion | flops 6447235072 | bytes 33558528 | tf_op jit(solution)/shard_map/rbk,kj->rbj/dot_general | solution.py:34
  136.5 0.0 reduce-scatter.2.cloned.1.call-update
  136.5 0.0 all-gather.2.cloned.1.call-done
  136.6 12.8 %fusion.2 = f32[512,1024]{1,0:T(8,128)} fusion(bf16[4096,1024]{1,0:T(8,128)(2,1)} %all-gather.2.cloned.1.call-done, bf16[4096,1024]{1,0:T(8,128)(2,1)} %param.10, bf16[512,8192]{1,0:T(8,128)(2,1)} %copy-done.4, s32[]{:T(128)S(6)} %select_n.22), kind=kOutput, calls=%fused_computation.3 | convolution fusion | flops 4311744512 | bytes 23068676 | tf_op jit(solution)/shard_map/dot_general | solution.py:61
  149.4 157.6 %reduce-scatter.2.cloned.1.call-done = f32[512,1024]{0,1:T(8,128)} async-done(((f32[4096,1024]{0,1:T(8,128)}), f32[512,1024]{0,1:T(8,128)}) %reduce-scatter.2.cloned.1.call-update) | async-done | bytes 2097168 | tf_op jit(solution)/shard_map/reduce_scatter | solution.py:64
  307.0 5.2 %convolution_multiply_fusion = f32[512,8,128]{0,2,1:T(8,128)} fusion(f32[512,8,128]{0,2,1:T(8,128)} %bitcast.15, f32[8,128]{1,0:T(8,128)S(1)} %convert_bitcast_fusion), kind=kOutput, calls=%fused_computation.14 | convolution fusion | flops 806420480 | bytes 4198400 | tf_op jit(solution)/shard_map/rbj,jk->rbk/dot_general | solution.py:41
  312.2 1.9 copy.19
  314.1 0.0 copy-start.3
  314.1 0.0 copy-start.1
  314.1 6.9 %multiply_subtract_fusion = (f32[512,1024]{1,0:T(8,128)}, f32[512,1024]{1,0:T(8,128)}, f32[512,1024]{1,0:T(8,128)}) fusion(f32[512,1024]{1,0:T(8,128)} %param.13, f32[512,1024]{1,0:T(8,128)S(1)} %copy.19, f32[512,1024]{1,0:T(8,128)} %param.14, f32[512,1024]{1,0:T(8,128)} %param.15), kind=kLoop, calls=%fused_computation.12 | loop fusion | flops 7864320 | bytes 14680064 | tf_op jit(solution)/shard_map/sub | solution.py:73
  321.0 0.0 copy-done.3
  321.0 0.9 abs_reduce_fusion
  321.9 0.0 copy-done.1
  (1 shorter events, 0.0 us)
Async XLA Ops:
  7.2 80.8 %copy-start = (bf16[512,1024]{1,0:T(8,128)(2,1)S(1)}, bf16[512,1024]{1,0:T(8,128)(2,1)}, u32[]{:S(2)}) copy-start(bf16[512,1024]{1,0:T(8,128)(2,1)} %param.9) | copy-start | bytes 3145732
  7.2 129.4 %all-gather.2.cloned.1.call-start = ((), (), s32[]{:S(2)}) async-start(), calls=%async_computation.1 | async-start | bytes 9437184 | tf_op jit(solution)/shard_map/all_gather | solution.py:58
  7.9 30.9 %copy-start.2 = (bf16[512,1024]{1,0:T(8,128)(2,1)S(1)}, bf16[512,1024]{1,0:T(8,128)(2,1)}, u32[]{:S(2)}) copy-start(bf16[512,1024]{1,0:T(8,128)(2,1)} %param.8) | copy-start | bytes 3145732
  7.9 299.1 %reduce-scatter.2.cloned.1.call-start = ((), (), s32[]{:S(2)}) async-start(), calls=%async_computation.2 | async-start | bytes 18874368 | tf_op jit(solution)/shard_map/reduce_scatter | solution.py:64
  8.0 26.7 %collective-permute-start = (bf16[512,1024]{1,0:T(8,128)(2,1)}, bf16[512,1024]{1,0:T(8,128)(2,1)S(1)}, u32[]{:S(2)}, u32[]{:S(2)}) collective-permute-start(bf16[512,1024]{1,0:T(8,128)(2,1)} %param.8), channel_id=1, source_target_pairs={{0,24},{8,0},{16,8},{24,16},{1,25},{9,1},{17,9},{25,17},{2,26},{10... | collective-permute-start | bytes 3145736 | tf_op jit(solution)/shard_map/ppermute | solution.py:14
  37.4 1.6 copy-start.5
  37.4 46.9 %collective-permute-start.1 = (bf16[512,2048]{1,0:T(8,128)(2,1)}, bf16[512,2048]{1,0:T(8,128)(2,1)}, u32[]{:S(2)}, u32[]{:S(2)}) collective-permute-start(bf16[512,2048]{1,0:T(8,128)(2,1)} %pad_maximum_fusion), channel_id=1, source_target_pairs={{0,16},{8,24},{16,0},{24,8},{1,17},{9,25},{17,1},{25,9},{2,18},{10... | collective-permute-start | bytes 6291464 | tf_op jit(solution)/shard_map/ppermute | solution.py:14
  88.0 8.3 %copy-start.4 = (bf16[512,8192]{1,0:T(8,128)(2,1)}, bf16[512,8192]{1,0:T(8,128)(2,1)S(1)}, u32[]{:S(2)}) copy-start(bf16[512,8192]{1,0:T(8,128)(2,1)S(1)} %constant_dynamic-update-slice_fusion) | copy-start | bytes 25165828
  314.1 6.9 %copy-start.3 = (f32[512,1024]{0,1:T(8,128)S(1)}, f32[512,1024]{0,1:T(8,128)}, u32[]{:S(2)}) copy-start(f32[512,1024]{0,1:T(8,128)} %reduce-scatter.2.cloned.1.call-done) | copy-start | bytes 6291460
  314.1 7.8 %copy-start.1 = (bf16[512,1024]{1,0:T(8,128)(2,1)S(1)}, bf16[512,1024]{1,0:T(8,128)(2,1)}, u32[]{:S(2)}) copy-start(bf16[512,1024]{1,0:T(8,128)(2,1)} %param.9) | copy-start | bytes 3145732
Sparse Core Ops, SparseCore 0:
  9.6 84.7 all-gather.1
  136.7 170.2 reduce-scatter.1
